TPU v7x, 32 devices: a whole 2x2x4 slice. The times are simulated.
32 devices in a mesh: ctx: 8 (over z, y), tile: 4 (over x, core).
Axes of the slice: x: 2, y: 2, z: 4, core: 2. Of those that a mesh axis runs over, the one named last changes fastest.
Arguments:
- masks: bfloat16 [16, 512, 512], P('ctx', 'tile'), may hold values from 0 to 1
- blur_rows: bfloat16 [512, 512], replicated, may hold values from -0.25 to 0.25
- blur_cols: bfloat16 [512, 512], replicated, may hold values from -0.25 to 0.25
- pupils: float32 [6, 64, 128], replicated, may hold values from -5 to 5
- targets: bfloat16 [16, 512, 512], P('ctx', 'tile'), may hold values from 0 to 1
- context_masters: int32 [16, 12], P('ctx'), may hold values from 0 to 15, as said below
- offsets: int32 [16, 12, 2], P('ctx'), may hold values from 0 to 511
Outputs:
- resist: bfloat16 [16, 512, 512], P('ctx', 'tile')
- mask_grad: float32 [16, 512, 512], P('ctx', 'tile')
Inputs may be any that keep to these rules, and one draw needn't show every extreme that they name: `context_masters`: master m lies on ctx index m // 2. Among the masters named by the 2 contexts of one ctx index there is at most one lying on any one ctx index; a master may be named several times.
All inputs are finite; a program needn't handle non-finite values.
Results may differ from a plain program's by a relative error of at most 0.019.
Values may be sent and summed in bfloat16 or wider, within the bound.
No kernel may reach another device: no remote copies, remote signals or barrier semaphores. Data moves between devices by JAX's collectives and lax.ppermute only.
A program may use at most 64 MiB of HBM per device.

v0:
```python
import math
import jax
import jax.numpy as jnp
from jax import lax
from jax.sharding import PartitionSpec as P

STEEPNESS = 4.0
THRESHOLD = 1.0


def build_tables(extent, mode_count):
    frequency = (jnp.arange(mode_count, dtype=jnp.int32) - mode_count // 2) % extent
    positions = jnp.arange(extent, dtype=jnp.int32)
    windings = frequency[:, None] * positions[None, :] % extent
    angles = windings.astype(jnp.float32) * (2.0 * math.pi / extent)
    scale_factor = 1.0 / math.sqrt(extent)
    cosine_table = jnp.cos(angles) * scale_factor
    sine_table = jnp.sin(angles) * scale_factor
    row_real = cosine_table.astype(jnp.bfloat16)
    row_imag = (-sine_table).astype(jnp.bfloat16)
    col_fwd = jnp.concatenate([cosine_table.T, -sine_table.T], axis=1).astype(jnp.bfloat16)
    inverse_big = jnp.concatenate(
        [
            jnp.concatenate([cosine_table, sine_table], axis=1),
            jnp.concatenate([-sine_table, cosine_table], axis=1),
        ],
        axis=0,
    ).astype(jnp.bfloat16)
    back_real = cosine_table.T.astype(jnp.bfloat16)
    back_imag = sine_table.T.astype(jnp.bfloat16)
    adjoint_big = jnp.concatenate(
        [
            jnp.concatenate([cosine_table.T, -sine_table.T], axis=1),
            jnp.concatenate([sine_table.T, cosine_table.T], axis=1),
        ],
        axis=0,
    ).astype(jnp.bfloat16)
    return (row_real, row_imag, col_fwd, inverse_big, back_real, back_imag, adjoint_big)


def complex_left(left_real, left_imag, values):
    width = values.shape[-1] // 2
    real_lead = jnp.einsum("ux,...xv->...uv", left_real, values, preferred_element_type=jnp.float32)
    imag_lead = jnp.einsum("ux,...xv->...uv", left_imag, values, preferred_element_type=jnp.float32)
    return jnp.concatenate(
        [
            real_lead[..., :width] - imag_lead[..., width:],
            real_lead[..., width:] + imag_lead[..., :width],
        ],
        axis=-1,
    )


def complex_times(factor, values, conjugate):
    width = values.shape[-1] // 2
    factor_real = factor[..., :width]
    factor_imag = factor[..., width:]
    if conjugate:
        factor_imag = -factor_imag
    values_real = values[..., :width]
    values_imag = values[..., width:]
    return jnp.concatenate(
        [
            factor_real * values_real - factor_imag * values_imag,
            factor_real * values_imag + factor_imag * values_real,
        ],
        axis=-1,
    )


def phase_table(shifts, row_begin, band_rows, mode_count, extent):
    freq_u = (jnp.arange(band_rows, dtype=jnp.int32) + row_begin - mode_count // 2) % extent
    freq_v = (jnp.arange(mode_count, dtype=jnp.int32) - mode_count // 2) % extent
    windings = (
        freq_u[None, :, None] * shifts[:, 0][:, None, None]
        + freq_v[None, None, :] * shifts[:, 1][:, None, None]
    ) % extent
    angles = windings.astype(jnp.float32) * (2.0 * math.pi / extent)
    return jnp.concatenate([jnp.cos(angles), -jnp.sin(angles)], axis=-1)


def image_adjoint(
    spectrum, target, pupils, back_real, back_imag, row_real, row_imag, inverse_big, adjoint_big
):
    amplitude = complex_times(pupils, spectrum[None], False).astype(jnp.bfloat16)
    spread = jnp.einsum(
        "kuv,vy->kuy", amplitude, inverse_big, preferred_element_type=jnp.float32
    ).astype(jnp.bfloat16)
    field = complex_left(back_real, back_imag, spread)
    width = field.shape[-1] // 2
    field_real = field[..., :width]
    field_imag = field[..., width:]
    intensity = jnp.sum(field_real * field_real + field_imag * field_imag, axis=0)
    resist = jax.nn.sigmoid(STEEPNESS * (intensity - THRESHOLD))
    slope_term = (resist - target.astype(jnp.float32)) * STEEPNESS * resist * (1.0 - resist)
    pull_back = jnp.concatenate(
        [2.0 * slope_term * field_real, 2.0 * slope_term * field_imag], axis=-1
    ).astype(jnp.bfloat16)
    folded = jnp.einsum(
        "kxy,yv->kxv", pull_back, adjoint_big, preferred_element_type=jnp.float32
    ).astype(jnp.bfloat16)
    grad_amp = complex_left(row_real, row_imag, folded)
    grad_spec = jnp.sum(complex_times(pupils, grad_amp, True), axis=0)
    return (resist.astype(jnp.bfloat16), grad_spec)


def local(masks, blur_rows, blur_cols, pupils, targets, context_masters, offsets):
    ctx_count = lax.axis_size("ctx")
    owned, row_count, extent = masks.shape
    mode_count = pupils.shape[1]
    context_count = context_masters.shape[0]
    source_count = context_masters.shape[1]
    tile_pos = lax.axis_index("tile")
    row_start = tile_pos * row_count
    row_real, row_imag, col_fwd, inverse_big, back_real, back_imag, adjoint_big = build_tables(
        extent, mode_count
    )
    own_row_real = lax.dynamic_slice_in_dim(row_real, row_start, row_count, 1)
    own_row_imag = lax.dynamic_slice_in_dim(row_imag, row_start, row_count, 1)
    own_back_real = lax.dynamic_slice_in_dim(back_real, row_start, row_count, 0)
    own_back_imag = lax.dynamic_slice_in_dim(back_imag, row_start, row_count, 0)
    own_blur = lax.dynamic_slice_in_dim(blur_rows, row_start, row_count, 0)
    own_blur_cols = lax.dynamic_slice_in_dim(blur_rows, row_start, row_count, 1)
    owners = (context_masters // owned).reshape(-1)
    local_index = (context_masters % owned).reshape(-1)
    slot_index = jnp.arange(ctx_count, dtype=jnp.int32)
    owner_match = owners[:, None] == slot_index[None, :]
    wanted = jnp.max(jnp.where(owner_match, local_index[:, None] + 1, 0), axis=0)
    asked_for = lax.all_to_all(wanted[:, None], "ctx", split_axis=0, concat_axis=0, tiled=True)[
        :, 0
    ]
    chosen = asked_for[:, None] == jnp.arange(owned, dtype=jnp.int32)[None, :] + 1
    half_blur = jnp.einsum(
        "mxy,zy->mxz", masks, blur_cols, preferred_element_type=jnp.float32
    ).astype(jnp.bfloat16)
    weights = own_blur
    blurred = jnp.einsum(
        "xj,mjz->mxz",
        weights,
        lax.all_gather(half_blur, "tile", axis=1, tiled=True),
        preferred_element_type=jnp.float32,
    ).astype(jnp.bfloat16)
    column = jnp.einsum("mxy,yv->mxv", blurred, col_fwd, preferred_element_type=jnp.float32).astype(
        jnp.bfloat16
    )
    partial_value = complex_left(own_row_real, own_row_imag, column)
    spectra = lax.psum(partial_value.astype(jnp.bfloat16), "tile")
    outgoing = jnp.einsum(
        "dm,muv->duv", chosen.astype(jnp.bfloat16), spectra, preferred_element_type=jnp.float32
    ).astype(jnp.bfloat16)
    incoming = lax.all_to_all(outgoing, "ctx", split_axis=0, concat_axis=0, tiled=True)
    flat_shift = offsets.reshape(-1, 2)
    picked = jnp.take(incoming, owners, axis=0).astype(jnp.float32)
    turned = complex_times(
        phase_table(flat_shift, 0, mode_count, mode_count, extent), picked, False
    )
    context_spec = jnp.sum(
        turned.reshape(context_count, source_count, mode_count, 2 * mode_count), axis=1
    )

    def one_context(inputs):
        spectrum, target = inputs
        return image_adjoint(
            spectrum,
            target,
            pupils,
            own_back_real,
            own_back_imag,
            own_row_real,
            own_row_imag,
            inverse_big,
            adjoint_big,
        )

    resist, grad_part = lax.map(one_context, (context_spec, targets))
    grad_ctx = lax.psum(grad_part.astype(jnp.bfloat16), "tile").astype(jnp.float32)
    band_start = 0
    repeated = jnp.repeat(grad_ctx, source_count, axis=0)
    back_turn = complex_times(
        phase_table(flat_shift, band_start, mode_count, mode_count, extent), repeated, True
    )
    returned = jnp.einsum(
        "rd,ruv->duv", owner_match.astype(jnp.float32), back_turn, precision=lax.Precision.HIGHEST
    )
    arrived = lax.all_to_all(
        returned.astype(jnp.bfloat16), "ctx", split_axis=0, concat_axis=0, tiled=True
    ).astype(returned.dtype)
    master_grad = jnp.einsum(
        "dm,duv->muv", chosen.astype(jnp.float32), arrived, precision=lax.Precision.HIGHEST
    ).astype(jnp.bfloat16)
    lifted = jnp.einsum(
        "muv,vy->muy", master_grad, inverse_big, preferred_element_type=jnp.float32
    ).astype(jnp.bfloat16)
    surface = (
        jnp.einsum(
            "xu,muy->mxy", own_back_real, lifted[..., :extent], preferred_element_type=jnp.float32
        )
        - jnp.einsum(
            "xu,muy->mxy", own_back_imag, lifted[..., extent:], preferred_element_type=jnp.float32
        )
    ).astype(jnp.bfloat16)
    settled = jnp.einsum(
        "mxy,yz->mxz", surface, blur_cols, preferred_element_type=jnp.float32
    ).astype(jnp.bfloat16)
    weights = own_blur_cols
    mask_grad = jnp.einsum(
        "jx,mjz->mxz",
        weights,
        lax.all_gather(settled, "tile", axis=1, tiled=True),
        preferred_element_type=jnp.float32,
    )
    return (resist, mask_grad)


def solution(mesh):
    placed = (
        P("ctx", "tile", None),
        P(),
        P(),
        P(),
        P("ctx", "tile", None),
        P("ctx", None),
        P("ctx", None, None),
    )
    return jax.shard_map(
        local,
        mesh=mesh,
        in_specs=placed,
        out_specs=(P("ctx", "tile", None), P("ctx", "tile", None)),
        check_vma=False,
    )
```

profile of v0, /device:TPU:0, one launch (start us, length us, event | category | flops | bytes accessed | tf_op | source)
XLA Modules:
  0.0 133.8 jit_solution(16642103256916884030)
XLA Ops:
  7.2 1.0 copy-done
  8.2 2.0 %convolution_convert_fusion.4 = bf16[2,128,512]{2,1,0:T(8,128)(2,1)} fusion(bf16[2,128,512]{2,1,0:T(8,128)(2,1)} %param.9, bf16[512,512]{1,0:T(8,128)(2,1)S(1)} %copy-done), kind=kOutput, calls=%fused_computation.57 | convolution fusion | flops 134348800 | bytes 1048576 | tf_op jit(solution)/shard_map/mxy,zy->mxz/dot_general | solution.py:133
  10.2 0.7 and_select_fusion.1
  11.3 0.7 copy.75
  11.9 7.3 %all-to-all-start = ((s32[8,1,1]{2,1,0:T(1,128)}), s32[8,1,1]{2,1,0:T(1,128)S(1)}, u32[]{:S(2)}, u32[]{:S(2)}) async-start(s32[8,1,1]{2,1,0:T(1,128)} %copy.75), calls=%async_computation | async-start | bytes 8192 | tf_op jit(solution)/shard_map/all_to_all | solution.py:129
  19.3 0.7 copy.73
  20.1 1.1 fusion.45
  22.2 1.1 cosine_multiply_fusion
  23.7 2.0 %all-to-all-done = s32[8,1,1]{2,1,0:T(1,128)S(1)} async-done(((s32[8,1,1]{2,1,0:T(1,128)}), s32[8,1,1]{2,1,0:T(1,128)S(1)}, u32[]{:S(2)}, u32[]{:S(2)}) %all-to-all-start) | async-done | bytes 64 | tf_op jit(solution)/shard_map/all_to_all | solution.py:129
  26.0 3.9 %all-gather.3.cloned.1.call-done = bf16[2,512,512]{2,1,0:T(8,128)(2,1)} async-done(((bf16[2,128,512]{2,1,0:T(8,128)(2,1)}), bf16[2,512,512]{2,1,0:T(8,128)(2,1)}) %all-gather.3.cloned.1.call-update) | async-done | bytes 1048592 | tf_op jit(solution)/shard_map/all_gather | solution.py:140
  29.9 1.9 %fusion.26 = bf16[2,128,128]{2,1,0:T(8,128)(2,1)S(1)} fusion(bf16[2,512,512]{2,1,0:T(8,128)(2,1)} %all-gather.3.cloned.1.call-done, bf16[512,128]{1,0:T(8,128)(2,1)S(1)} %maximum_convert_fusion, bf16[512,512]{1,0:T(8,128)(2,1)S(1)} %copy-done.5, s32[]{:T(128)S(6)} %select_n.140), kind=kOutput, calls=%fused_computation.65 | convolution fusion | flops 167936000 | bytes 1376260 | tf_op jit(solution)/shard_map/mxy,yv->mxv/dot_general | solution.py:143
  32.3 10.4 %psum.14 = bf16[2,64,128]{2,1,0:T(8,128)(2,1)S(1)} all-reduce(bf16[2,64,128]{2,1,0:T(8,128)(2,1)S(1)} %pad_maximum_fusion.1), channel_id=1, replica_groups=mesh['ctx'=8,'tile'=4] {'tile'}, use_global_device_ids=true, to_apply=%region_1.2 | all-reduce | flops 16384 | bytes 65536 | tf_op jit(solution)/shard_map/psum | solution.py:147
  43.0 0.7 copy.79
  43.6 5.7 %all-to-all-start.1 = ((bf16[8,64,128]{2,1,0:T(8,128)(2,1)}), bf16[8,64,128]{2,1,0:T(8,128)(2,1)S(1)}, u32[]{:S(2)}, u32[]{:S(2)}) async-start(bf16[8,64,128]{2,1,0:T(8,128)(2,1)} %copy.79), calls=%async_computation.1 | async-start | bytes 262144 | tf_op jit(solution)/shard_map/all_to_all | solution.py:151
  49.5 7.2 %all-to-all-done.1 = bf16[8,64,128]{2,1,0:T(8,128)(2,1)S(1)} async-done(((bf16[8,64,128]{2,1,0:T(8,128)(2,1)}), bf16[8,64,128]{2,1,0:T(8,128)(2,1)S(1)}, u32[]{:S(2)}, u32[]{:S(2)}) %all-to-all-start.1) | async-done | bytes 131104 | tf_op jit(solution)/shard_map/all_to_all | solution.py:151
  57.6 4.6 %multiply_subtract_fusion.2 = (f32[24,64,64]{2,0,1:T(8,128)S(1)}, f32[24,64,64]{2,0,1:T(8,128)S(1)}) fusion(f32[24,64,128]{2,0,1:T(8,128)S(1)} %fusion.35, s32[24,64]{1,0:T(8,128)S(1)} %get-tuple-element.289, s32[24,64]{0,1:T(8,128)S(1)} %copy.74), kind=kLoop, calls=%fused_computation.79 | loop fusion | flops 2064384 | bytes 1585152 | tf_op jit(solution)/shard_map/sub | solution.py:64
  62.7 0.7 copy-done.4
  63.4 19.3 %while.14 = (s32[]{:T(128)}, bf16[2,128,512]{2,1,0:T(8,128)(2,1)}, bf16[2,64,128]{2,1,0:T(8,128)(2,1)S(1)}, f32[6,64,128]{2,1,0:T(8,128)S(1)}, f32[2,64,128]{2,1...) while((s32[]{:T(128)}, bf16[2,128,512]{2,1,0:T(8,128)(2,1)}, ...), condition=%wide.region_6.7_spmd, body=%wide.region_3.6_spmd.sunk | while | flops 538632192 | bytes 57360672 | solution.py:175
  64.7 0.6 convolution_bitcast_fusion.12
  65.3 1.0 copy-done.1
  66.8 1.2 copy-done.2
  68.5 3.3 %multiply_convert_fusion.4 = (bf16[6,128,512]{1,2,0:T(8,128)(2,1)S(1)}, bf16[6,128,512]{1,2,0:T(8,128)(2,1)S(1)}) fusion(f32[128,512]{0,1:T(8,128)S(1)} %fusion.130, f32[6,128,1024]{1,2,0:T(8,128)} %copy-done.1, f32[6,128,1024]{1,2,0:T(8,128)} %copy-done.2), kind=kLoop, calls=%fused_computation.10.clone.1 | loop fusion | flops 2359296 | bytes 8126464 | tf_op jit(solution)/shard_map/convert
  75.0 1.0 copy-done.1
  76.4 1.2 copy-done.2
  78.2 3.3 %multiply_convert_fusion.4 = (bf16[6,128,512]{1,2,0:T(8,128)(2,1)S(1)}, bf16[6,128,512]{1,2,0:T(8,128)(2,1)S(1)}) fusion(f32[128,512]{0,1:T(8,128)S(1)} %fusion.130, f32[6,128,1024]{1,2,0:T(8,128)} %copy-done.1, f32[6,128,1024]{1,2,0:T(8,128)} %copy-done.2), kind=kLoop, calls=%fused_computation.10.clone.1 | loop fusion | flops 2359296 | bytes 8126464 | tf_op jit(solution)/shard_map/convert
  82.8 10.4 %psum.15 = bf16[2,64,128]{2,1,0:T(8,128)(2,1)S(1)} all-reduce(bf16[2,64,128]{2,1,0:T(8,128)(2,1)S(1)} %get-tuple-element.159), channel_id=1, replica_groups=mesh['ctx'=8,'tile'=4] {'tile'}, use_global_device_ids=true, to_apply=%region_7.8 | all-reduce | flops 16384 | bytes 65536 | tf_op jit(solution)/shard_map/psum | solution.py:176
  93.6 3.7 %multiply_subtract_fusion.1 = (f32[24,64,64]{2,0,1:T(8,128)S(1)}, f32[24,64,64]{2,0,1:T(8,128)S(1)}) fusion(f32[24,64,64]{2,1,0:T(8,128)S(1)} %get-tuple-element.276, f32[24,64,64]{2,1,0:T(8,128)S(1)} %get-tuple-element.275, s32[24,64]{1,0:T(8,128)S(1)} %get-tuple-element.289, s32[24,64]{0,1:T(8,128)S(1)} %copy.74), kind=kLoop, calls=%fused_computation.77 | loop fusion | flops 1966080 | bytes 1585152 | tf_op jit(solution)/shard_map/sub | solution.py:64
  97.8 9.9 %all_to_all.19 = bf16[8,64,128]{2,1,0:T(8,128)(2,1)S(1)} all-to-all(bf16[8,64,128]{2,1,0:T(8,128)(2,1)S(1)} %copy.87), channel_id=1, replica_groups=mesh['ctx'=8,'tile'=4] {'ctx'}, dimensions={0} | all-to-all | bytes 262144 | tf_op jit(solution)/shard_map/all_to_all | solution.py:185
  108.5 1.3 %convolution_convert_fusion.1 = bf16[2,128,512]{2,1,0:T(8,128)(2,1)} fusion(f32[2,512,128]{2,1,0:T(8,128)S(1)} %fusion.52, bf16[512,512]{1,0:T(8,128)(2,1)S(1)} %copy-done, bf16[2,64,1024]{2,1,0:T(8,128)(2,1)S(1)} %convolution_convert_fusion.2, bf16[128,64]{1,0:T(8,128)(2,1)S(1)} %constant_dynamic-slice_fusion.1), kind=kOutput, calls=%fused_computation.54 | convolution fusion | flops 151388160 | bytes 1474560 | tf_op jit(solution)/shard_map/mxy,yz->mxz/dot_general | solution.py:202
  109.8 14.5 %all-gather.5.cloned.1.call-done = bf16[2,512,512]{2,1,0:T(8,128)(2,1)} async-done(((bf16[2,128,512]{2,1,0:T(8,128)(2,1)}), bf16[2,512,512]{2,1,0:T(8,128)(2,1)}) %all-gather.5.cloned.1.call-update) | async-done | bytes 1048592 | tf_op jit(solution)/shard_map/all_gather | solution.py:209
  124.3 1.7 %convolution_bitcast_fusion.4 = f32[2,128,512]{1,2,0:T(8,128)S(1)} fusion(bf16[2,512,512]{2,1,0:T(8,128)(2,1)} %all-gather.5.cloned.1.call-done, bf16[512,512]{1,0:T(8,128)(2,1)S(1)} %copy-done.5, s32[]{:T(128)S(6)} %select_n.140), kind=kOutput, calls=%fused_computation.51 | convolution fusion | flops 134217728 | bytes 1703940 | tf_op jit(solution)/shard_map/jx,mjz->mxz/dot_general | solution.py:206
  126.0 1.0 copy.95
  (98 shorter events, 13.3 us)
Async XLA Ops:
  7.2 1.0 copy-start
  7.2 22.7 %all-gather.3.cloned.1.call-start = ((), (), s32[]{:S(2)}) async-start(), calls=%async_computation.3 | async-start | bytes 1310720 | tf_op jit(solution)/shard_map/all_gather | solution.py:140
  10.2 19.7 %copy-start.5 = (bf16[512,512]{1,0:T(8,128)(2,1)S(1)}, bf16[512,512]{1,0:T(8,128)(2,1)}, u32[]{:S(2)}) copy-start(bf16[512,512]{1,0:T(8,128)(2,1)} %param.10) | copy-start | bytes 1572868
  11.9 13.8 %all-to-all-start = ((s32[8,1,1]{2,1,0:T(1,128)}), s32[8,1,1]{2,1,0:T(1,128)S(1)}, u32[]{:S(2)}, u32[]{:S(2)}) async-start(s32[8,1,1]{2,1,0:T(1,128)} %copy.75), calls=%async_computation | async-start | bytes 8192 | tf_op jit(solution)/shard_map/all_to_all | solution.py:129
  23.6 25.8 %copy-start.3 = (f32[6,64,128]{2,1,0:T(8,128)S(1)}, f32[6,64,128]{2,1,0:T(8,128)}, u32[]{:S(2)}) copy-start(f32[6,64,128]{2,1,0:T(8,128)} %param.12) | copy-start | bytes 589828
  43.6 13.0 %all-to-all-start.1 = ((bf16[8,64,128]{2,1,0:T(8,128)(2,1)}), bf16[8,64,128]{2,1,0:T(8,128)(2,1)S(1)}, u32[]{:S(2)}, u32[]{:S(2)}) async-start(bf16[8,64,128]{2,1,0:T(8,128)(2,1)} %copy.79), calls=%async_computation.1 | async-start | bytes 262144 | tf_op jit(solution)/shard_map/all_to_all | solution.py:151
  49.3 75.0 %all-gather.5.cloned.1.call-start = ((), (), s32[]{:S(2)}) async-start(), calls=%async_computation.4 | async-start | bytes 1310720 | tf_op jit(solution)/shard_map/all_gather | solution.py:209
  62.5 1.0 copy-start.4
  64.7 1.6 %copy-start.1 = (f32[6,128,1024]{1,2,0:T(8,128)}, f32[6,128,1024]{1,2,0:T(8,128)S(1)}, u32[]{:S(2)}) copy-start(f32[6,128,1024]{1,2,0:T(8,128)S(1)} %convolution_bitcast_fusion.11) | copy-start | bytes 9437188 | tf_op jit(solution)/shard_map/while
  66.3 1.7 %copy-start.2 = (f32[6,128,1024]{1,2,0:T(8,128)}, f32[6,128,1024]{1,2,0:T(8,128)S(1)}, u32[]{:S(2)}) copy-start(f32[6,128,1024]{1,2,0:T(8,128)S(1)} %convolution_bitcast_fusion.12) | copy-start | bytes 9437188 | tf_op jit(solution)/shard_map/while
  66.3 1.9 %copy-start.6 = (bf16[2,128,512]{2,1,0:T(8,128)(2,1)S(1)}, bf16[2,128,512]{2,1,0:T(8,128)(2,1)}, u32[]{:S(2)}) copy-start(bf16[2,128,512]{2,1,0:T(8,128)(2,1)} %get-tuple-element.410) | copy-start | bytes 786436 | tf_op jit(solution)/shard_map/while
  68.2 3.6 %copy-start.7 = (bf16[2,128,512]{2,1,0:T(8,128)(2,1)}, bf16[2,128,512]{2,1,0:T(8,128)(2,1)S(1)}, u32[]{:S(2)}) copy-start(bf16[2,128,512]{2,1,0:T(8,128)(2,1)S(1)} %get-tuple-element.426) | copy-start | bytes 786436 | tf_op jit(solution)/shard_map/while
  74.4 1.6 %copy-start.1 = (f32[6,128,1024]{1,2,0:T(8,128)}, f32[6,128,1024]{1,2,0:T(8,128)S(1)}, u32[]{:S(2)}) copy-start(f32[6,128,1024]{1,2,0:T(8,128)S(1)} %convolution_bitcast_fusion.11) | copy-start | bytes 9437188 | tf_op jit(solution)/shard_map/while
  76.0 1.7 %copy-start.2 = (f32[6,128,1024]{1,2,0:T(8,128)}, f32[6,128,1024]{1,2,0:T(8,128)S(1)}, u32[]{:S(2)}) copy-start(f32[6,128,1024]{1,2,0:T(8,128)S(1)} %convolution_bitcast_fusion.12) | copy-start | bytes 9437188 | tf_op jit(solution)/shard_map/while
  76.0 1.9 %copy-start.6 = (bf16[2,128,512]{2,1,0:T(8,128)(2,1)S(1)}, bf16[2,128,512]{2,1,0:T(8,128)(2,1)}, u32[]{:S(2)}) copy-start(bf16[2,128,512]{2,1,0:T(8,128)(2,1)} %get-tuple-element.410) | copy-start | bytes 786436 | tf_op jit(solution)/shard_map/while
  77.9 3.6 %copy-start.7 = (bf16[2,128,512]{2,1,0:T(8,128)(2,1)}, bf16[2,128,512]{2,1,0:T(8,128)(2,1)S(1)}, u32[]{:S(2)}) copy-start(bf16[2,128,512]{2,1,0:T(8,128)(2,1)S(1)} %get-tuple-element.426) | copy-start | bytes 786436 | tf_op jit(solution)/shard_map/while
Sparse Core Ops, SparseCore 0:
  10.3 19.4 all-gather.2
  110.0 14.2 all-gather.4
where the time goes:
time: 134 us
  blocking collectives  30.8 us (23%)
  waiting for transfers between devices  27.6 us (21%)
  other arithmetic  22.2 us (17%)
  between operations  14.3 us (11%)
  matrix products  13.9 us (10%)
  starting transfers between devices  13.1 us (10%)
  local copies, waits for them, and re-layouts  11.7 us (9%)
    all_gather x1, waiting for transfers between devices, local(): lax.all_gather(settled, 'tile', axis=1, tiled=True)  14.5 us
    psum x1, blocking collectives, local(): lax.psum(grad_part.astype(jnp.bfloat16), 'tile').astype(jnp.float32)  10.4 us
    psum x1, blocking collectives, local(): spectra = lax.psum(partial_value.astype(jnp.bfloat16), 'tile')  10.4 us
    all_to_all x1, blocking collectives, local(): lax.all_to_all(returned.astype(jnp.bfloat16), 'ctx', split_axis=0, concat...  9.92 us
    sub x4, other arithmetic, complex_times(): factor_real * values_real - factor_imag * values_imag  8.65 us
    another operation x6, other arithmetic  7.55 us
    all_to_all x1, starting transfers between devices, local(): lax.all_to_all(wanted[:, None], 'ctx', split_axis=0, concat_axis=0, tiled...  7.31 us
    all_to_all x1, waiting for transfers between devices, local(): lax.all_to_all(outgoing, 'ctx', split_axis=0, concat_axis=0, tiled=True)  7.17 us
  transfers between devices with their start and end apart: 4, of which 4 were waited for; matrix products, arithmetic and copies ran while one was open for 5% of the time, Pallas kernels for 0%

commit v1 on v0

--- a/solution.py
+++ b/solution.py
@@ -6,6 +6,12 @@
 
 STEEPNESS = 4.0
 THRESHOLD = 1.0
+
+
+def gather_and_add(x, mesh_axis):
+    terms = lax.all_gather(x, mesh_axis, axis=0, tiled=False)
+    summed = terms.sum(axis=0)
+    return summed
 
 
 def build_tables(extent, mode_count):
@@ -173,7 +179,7 @@
         )
 
     resist, grad_part = lax.map(one_context, (context_spec, targets))
-    grad_ctx = lax.psum(grad_part.astype(jnp.bfloat16), "tile").astype(jnp.float32)
+    grad_ctx = gather_and_add(grad_part.astype(jnp.bfloat16), "tile").astype(jnp.float32)
     band_start = 0
     repeated = jnp.repeat(grad_ctx, source_count, axis=0)
     back_turn = complex_times(

time: 134 us -> 130 us (0.970)
  blocking collectives: 30.8 us -> 26.1 us
    psum x1 -> x0, blocking collectives: 10.4 us -> none  [local(): lax.psum(grad_part.astype(jnp.bfloat16), 'tile').astype(jnp.float32)]
    all_gather x0 -> x1, blocking collectives: none -> 5.6 us  [gather_and_add(): terms = lax.all_gather(x, mesh_axis, axis=0, tiled=False)]
where the time goes in v1:
time: 130 us
  waiting for transfers between devices  28.1 us (22%)
  blocking collectives  26.1 us (20%)
  other arithmetic  22.2 us (17%)
  between operations  14.3 us (11%)
  matrix products  13.9 us (11%)
  starting transfers between devices  13.1 us (10%)
  local copies, waits for them, and re-layouts  11.7 us (9%)
    all_gather x1, waiting for transfers between devices, local(): lax.all_gather(settled, 'tile', axis=1, tiled=True)  15 us
    psum x1, blocking collectives, local(): spectra = lax.psum(partial_value.astype(jnp.bfloat16), 'tile')  10.4 us
    all_to_all x1, blocking collectives, local(): lax.all_to_all(returned.astype(jnp.bfloat16), 'ctx', split_axis=0, concat...  10.2 us
    sub x4, other arithmetic, complex_times(): factor_real * values_real - factor_imag * values_imag  8.65 us
    another operation x6, other arithmetic  7.55 us
    all_to_all x1, starting transfers between devices, local(): lax.all_to_all(wanted[:, None], 'ctx', split_axis=0, concat_axis=0, tiled...  7.31 us
    all_to_all x1, waiting for transfers between devices, local(): lax.all_to_all(outgoing, 'ctx', split_axis=0, concat_axis=0, tiled=True)  7.17 us
    all_to_all x1, starting transfers between devices, local(): lax.all_to_all(outgoing, 'ctx', split_axis=0, concat_axis=0, tiled=True)  5.67 us
  transfers between devices with their start and end apart: 4, of which 4 were waited for; matrix products, arithmetic and copies ran while one was open for 5% of the time, Pallas kernels for 0%

profile of v1, /device:TPU:0, one launch (start us, length us, event | category | flops | bytes accessed | tf_op | source)
XLA Modules:
  0.0 129.7 jit_solution(12253264693569903342)
XLA Ops:
  7.2 1.0 copy-done
  8.2 2.0 %convolution_convert_fusion.4 = bf16[2,128,512]{2,1,0:T(8,128)(2,1)} fusion(bf16[2,128,512]{2,1,0:T(8,128)(2,1)} %param.9, bf16[512,512]{1,0:T(8,128)(2,1)S(1)} %copy-done), kind=kOutput, calls=%fused_computation.57 | convolution fusion | flops 134348800 | bytes 1048576 | tf_op jit(solution)/shard_map/mxy,zy->mxz/dot_general | solution.py:139
  10.2 0.7 and_select_fusion.1
  11.3 0.7 copy.74
  11.9 7.3 %all-to-all-start = ((s32[8,1,1]{2,1,0:T(1,128)}), s32[8,1,1]{2,1,0:T(1,128)S(1)}, u32[]{:S(2)}, u32[]{:S(2)}) async-start(s32[8,1,1]{2,1,0:T(1,128)} %copy.74), calls=%async_computation | async-start | bytes 8192 | tf_op jit(solution)/shard_map/all_to_all | solution.py:135
  19.3 0.7 copy.72
  20.1 1.1 fusion.45
  22.2 1.1 cosine_multiply_fusion
  23.7 2.0 %all-to-all-done = s32[8,1,1]{2,1,0:T(1,128)S(1)} async-done(((s32[8,1,1]{2,1,0:T(1,128)}), s32[8,1,1]{2,1,0:T(1,128)S(1)}, u32[]{:S(2)}, u32[]{:S(2)}) %all-to-all-start) | async-done | bytes 64 | tf_op jit(solution)/shard_map/all_to_all | solution.py:135
  26.0 3.9 %all-gather.4.cloned.1.call-done = bf16[2,512,512]{2,1,0:T(8,128)(2,1)} async-done(((bf16[2,128,512]{2,1,0:T(8,128)(2,1)}), bf16[2,512,512]{2,1,0:T(8,128)(2,1)}) %all-gather.4.cloned.1.call-update) | async-done | bytes 1048592 | tf_op jit(solution)/shard_map/all_gather | solution.py:146
  29.9 1.9 %fusion.26 = bf16[2,128,128]{2,1,0:T(8,128)(2,1)S(1)} fusion(bf16[2,512,512]{2,1,0:T(8,128)(2,1)} %all-gather.4.cloned.1.call-done, bf16[512,128]{1,0:T(8,128)(2,1)S(1)} %maximum_convert_fusion, bf16[512,512]{1,0:T(8,128)(2,1)S(1)} %copy-done.5, s32[]{:T(128)S(6)} %select_n.140), kind=kOutput, calls=%fused_computation.65 | convolution fusion | flops 167936000 | bytes 1376260 | tf_op jit(solution)/shard_map/mxy,yv->mxv/dot_general | solution.py:149
  32.3 10.4 %psum.7 = bf16[2,64,128]{2,1,0:T(8,128)(2,1)S(1)} all-reduce(bf16[2,64,128]{2,1,0:T(8,128)(2,1)S(1)} %pad_maximum_fusion.1), channel_id=1, replica_groups=mesh['ctx'=8,'tile'=4] {'tile'}, use_global_device_ids=true, to_apply=%region_1.2 | all-reduce | flops 16384 | bytes 65536 | tf_op jit(solution)/shard_map/psum | solution.py:153
  43.0 0.7 copy.78
  43.6 5.7 %all-to-all-start.1 = ((bf16[8,64,128]{2,1,0:T(8,128)(2,1)}), bf16[8,64,128]{2,1,0:T(8,128)(2,1)S(1)}, u32[]{:S(2)}, u32[]{:S(2)}) async-start(bf16[8,64,128]{2,1,0:T(8,128)(2,1)} %copy.78), calls=%async_computation.1 | async-start | bytes 262144 | tf_op jit(solution)/shard_map/all_to_all | solution.py:157
  49.5 7.2 %all-to-all-done.1 = bf16[8,64,128]{2,1,0:T(8,128)(2,1)S(1)} async-done(((bf16[8,64,128]{2,1,0:T(8,128)(2,1)}), bf16[8,64,128]{2,1,0:T(8,128)(2,1)S(1)}, u32[]{:S(2)}, u32[]{:S(2)}) %all-to-all-start.1) | async-done | bytes 131104 | tf_op jit(solution)/shard_map/all_to_all | solution.py:157
  57.6 4.6 %multiply_subtract_fusion.2 = (f32[24,64,64]{2,0,1:T(8,128)S(1)}, f32[24,64,64]{2,0,1:T(8,128)S(1)}) fusion(f32[24,64,128]{2,0,1:T(8,128)S(1)} %fusion.35, s32[24,64]{1,0:T(8,128)S(1)} %get-tuple-element.289, s32[24,64]{0,1:T(8,128)S(1)} %copy.73), kind=kLoop, calls=%fused_computation.79 | loop fusion | flops 2064384 | bytes 1585152 | tf_op jit(solution)/shard_map/sub | solution.py:70
  62.7 0.7 copy-done.4
  63.4 19.3 %while.14 = (s32[]{:T(128)}, bf16[2,128,512]{2,1,0:T(8,128)(2,1)}, bf16[2,64,128]{2,1,0:T(8,128)(2,1)S(1)}, f32[6,64,128]{2,1,0:T(8,128)S(1)}, f32[2,64,128]{2,1...) while((s32[]{:T(128)}, bf16[2,128,512]{2,1,0:T(8,128)(2,1)}, ...), condition=%wide.region_6.7_spmd, body=%wide.region_3.6_spmd.sunk | while | flops 538632192 | bytes 57360672 | solution.py:181
  64.7 0.6 convolution_bitcast_fusion.12
  65.3 1.0 copy-done.1
  66.8 1.2 copy-done.2
  68.5 3.3 %multiply_convert_fusion.4 = (bf16[6,128,512]{1,2,0:T(8,128)(2,1)S(1)}, bf16[6,128,512]{1,2,0:T(8,128)(2,1)S(1)}) fusion(f32[128,512]{0,1:T(8,128)S(1)} %fusion.130, f32[6,128,1024]{1,2,0:T(8,128)} %copy-done.1, f32[6,128,1024]{1,2,0:T(8,128)} %copy-done.2), kind=kLoop, calls=%fused_computation.10.clone.1 | loop fusion | flops 2359296 | bytes 8126464 | tf_op jit(solution)/shard_map/convert.1
  75.0 1.0 copy-done.1
  76.4 1.2 copy-done.2
  78.2 3.3 %multiply_convert_fusion.4 = (bf16[6,128,512]{1,2,0:T(8,128)(2,1)S(1)}, bf16[6,128,512]{1,2,0:T(8,128)(2,1)S(1)}) fusion(f32[128,512]{0,1:T(8,128)S(1)} %fusion.130, f32[6,128,1024]{1,2,0:T(8,128)} %copy-done.1, f32[6,128,1024]{1,2,0:T(8,128)} %copy-done.2), kind=kLoop, calls=%fused_computation.10.clone.1 | loop fusion | flops 2359296 | bytes 8126464 | tf_op jit(solution)/shard_map/convert.1
  82.8 5.6 %all-gather = bf16[8,64,128]{2,1,0:T(8,128)(2,1)S(1)} all-gather(bf16[2,64,128]{2,1,0:T(8,128)(2,1)S(1)} %get-tuple-element.159), channel_id=2, replica_groups=mesh['ctx'=8,'tile'=4] {'tile'}, dimensions={0}, use_global_device_ids=true | all-gather | bytes 163840 | tf_op jit(solution)/shard_map/all_gather | solution.py:12
  88.8 3.7 %multiply_subtract_fusion.1 = (f32[24,64,64]{2,0,1:T(8,128)S(1)}, f32[24,64,64]{2,0,1:T(8,128)S(1)}) fusion(f32[24,64,64]{2,1,0:T(8,128)S(1)} %get-tuple-element.276, f32[24,64,64]{2,1,0:T(8,128)S(1)} %get-tuple-element.275, s32[24,64]{1,0:T(8,128)S(1)} %get-tuple-element.289, s32[24,64]{0,1:T(8,128)S(1)} %copy.73), kind=kLoop, calls=%fused_computation.77 | loop fusion | flops 1966080 | bytes 1585152 | tf_op jit(solution)/shard_map/sub | solution.py:70
  93.0 10.2 %all_to_all.19 = bf16[8,64,128]{2,1,0:T(8,128)(2,1)S(1)} all-to-all(bf16[8,64,128]{2,1,0:T(8,128)(2,1)S(1)} %copy.86), channel_id=1, replica_groups=mesh['ctx'=8,'tile'=4] {'ctx'}, dimensions={0} | all-to-all | bytes 262144 | tf_op jit(solution)/shard_map/all_to_all | solution.py:191
  103.9 1.3 %convolution_convert_fusion.1 = bf16[2,128,512]{2,1,0:T(8,128)(2,1)} fusion(f32[2,512,128]{2,1,0:T(8,128)S(1)} %fusion.52, bf16[512,512]{1,0:T(8,128)(2,1)S(1)} %copy-done, bf16[2,64,1024]{2,1,0:T(8,128)(2,1)S(1)} %convolution_convert_fusion.2, bf16[128,64]{1,0:T(8,128)(2,1)S(1)} %constant_dynamic-slice_fusion.1), kind=kOutput, calls=%fused_computation.54 | convolution fusion | flops 151388160 | bytes 1474560 | tf_op jit(solution)/shard_map/mxy,yz->mxz/dot_general | solution.py:208
  105.2 15.0 %all-gather.6.cloned.1.call-done = bf16[2,512,512]{2,1,0:T(8,128)(2,1)} async-done(((bf16[2,128,512]{2,1,0:T(8,128)(2,1)}), bf16[2,512,512]{2,1,0:T(8,128)(2,1)}) %all-gather.6.cloned.1.call-update) | async-done | bytes 1048592 | tf_op jit(solution)/shard_map/all_gather | solution.py:215
  120.2 1.7 %convolution_bitcast_fusion.4 = f32[2,128,512]{1,2,0:T(8,128)S(1)} fusion(bf16[2,512,512]{2,1,0:T(8,128)(2,1)} %all-gather.6.cloned.1.call-done, bf16[512,512]{1,0:T(8,128)(2,1)S(1)} %copy-done.5, s32[]{:T(128)S(6)} %select_n.140), kind=kOutput, calls=%fused_computation.51 | convolution fusion | flops 134217728 | bytes 1703940 | tf_op jit(solution)/shard_map/jx,mjz->mxz/dot_general | solution.py:212
  121.9 1.0 copy.94
  (99 shorter events, 13.3 us)
Async XLA Ops:
  7.2 1.0 copy-start
  7.2 22.7 %all-gather.4.cloned.1.call-start = ((), (), s32[]{:S(2)}) async-start(), calls=%async_computation.3 | async-start | bytes 1310720 | tf_op jit(solution)/shard_map/all_gather | solution.py:146
  10.2 19.7 %copy-start.5 = (bf16[512,512]{1,0:T(8,128)(2,1)S(1)}, bf16[512,512]{1,0:T(8,128)(2,1)}, u32[]{:S(2)}) copy-start(bf16[512,512]{1,0:T(8,128)(2,1)} %param.10) | copy-start | bytes 1572868
  11.9 13.8 %all-to-all-start = ((s32[8,1,1]{2,1,0:T(1,128)}), s32[8,1,1]{2,1,0:T(1,128)S(1)}, u32[]{:S(2)}, u32[]{:S(2)}) async-start(s32[8,1,1]{2,1,0:T(1,128)} %copy.74), calls=%async_computation | async-start | bytes 8192 | tf_op jit(solution)/shard_map/all_to_all | solution.py:135
  23.6 25.8 %copy-start.3 = (f32[6,64,128]{2,1,0:T(8,128)S(1)}, f32[6,64,128]{2,1,0:T(8,128)}, u32[]{:S(2)}) copy-start(f32[6,64,128]{2,1,0:T(8,128)} %param.12) | copy-start | bytes 589828
  43.6 13.0 %all-to-all-start.1 = ((bf16[8,64,128]{2,1,0:T(8,128)(2,1)}), bf16[8,64,128]{2,1,0:T(8,128)(2,1)S(1)}, u32[]{:S(2)}, u32[]{:S(2)}) async-start(bf16[8,64,128]{2,1,0:T(8,128)(2,1)} %copy.78), calls=%async_computation.1 | async-start | bytes 262144 | tf_op jit(solution)/shard_map/all_to_all | solution.py:157
  49.3 70.9 %all-gather.6.cloned.1.call-start = ((), (), s32[]{:S(2)}) async-start(), calls=%async_computation.4 | async-start | bytes 1310720 | tf_op jit(solution)/shard_map/all_gather | solution.py:215
  62.5 1.0 copy-start.4
  64.7 1.6 %copy-start.1 = (f32[6,128,1024]{1,2,0:T(8,128)}, f32[6,128,1024]{1,2,0:T(8,128)S(1)}, u32[]{:S(2)}) copy-start(f32[6,128,1024]{1,2,0:T(8,128)S(1)} %convolution_bitcast_fusion.11) | copy-start | bytes 9437188 | tf_op jit(solution)/shard_map/while
  66.3 1.7 %copy-start.2 = (f32[6,128,1024]{1,2,0:T(8,128)}, f32[6,128,1024]{1,2,0:T(8,128)S(1)}, u32[]{:S(2)}) copy-start(f32[6,128,1024]{1,2,0:T(8,128)S(1)} %convolution_bitcast_fusion.12) | copy-start | bytes 9437188 | tf_op jit(solution)/shard_map/while
  66.3 1.9 %copy-start.6 = (bf16[2,128,512]{2,1,0:T(8,128)(2,1)S(1)}, bf16[2,128,512]{2,1,0:T(8,128)(2,1)}, u32[]{:S(2)}) copy-start(bf16[2,128,512]{2,1,0:T(8,128)(2,1)} %get-tuple-element.410) | copy-start | bytes 786436 | tf_op jit(solution)/shard_map/while
  68.2 3.6 %copy-start.7 = (bf16[2,128,512]{2,1,0:T(8,128)(2,1)}, bf16[2,128,512]{2,1,0:T(8,128)(2,1)S(1)}, u32[]{:S(2)}) copy-start(bf16[2,128,512]{2,1,0:T(8,128)(2,1)S(1)} %get-tuple-element.426) | copy-start | bytes 786436 | tf_op jit(solution)/shard_map/while
  74.4 1.6 %copy-start.1 = (f32[6,128,1024]{1,2,0:T(8,128)}, f32[6,128,1024]{1,2,0:T(8,128)S(1)}, u32[]{:S(2)}) copy-start(f32[6,128,1024]{1,2,0:T(8,128)S(1)} %convolution_bitcast_fusion.11) | copy-start | bytes 9437188 | tf_op jit(solution)/shard_map/while
  76.0 1.7 %copy-start.2 = (f32[6,128,1024]{1,2,0:T(8,128)}, f32[6,128,1024]{1,2,0:T(8,128)S(1)}, u32[]{:S(2)}) copy-start(f32[6,128,1024]{1,2,0:T(8,128)S(1)} %convolution_bitcast_fusion.12) | copy-start | bytes 9437188 | tf_op jit(solution)/shard_map/while
  76.0 1.9 %copy-start.6 = (bf16[2,128,512]{2,1,0:T(8,128)(2,1)S(1)}, bf16[2,128,512]{2,1,0:T(8,128)(2,1)}, u32[]{:S(2)}) copy-start(bf16[2,128,512]{2,1,0:T(8,128)(2,1)} %get-tuple-element.410) | copy-start | bytes 786436 | tf_op jit(solution)/shard_map/while
  77.9 3.6 %copy-start.7 = (bf16[2,128,512]{2,1,0:T(8,128)(2,1)}, bf16[2,128,512]{2,1,0:T(8,128)(2,1)S(1)}, u32[]{:S(2)}) copy-start(bf16[2,128,512]{2,1,0:T(8,128)(2,1)S(1)} %get-tuple-element.426) | copy-start | bytes 786436 | tf_op jit(solution)/shard_map/while
Sparse Core Ops, SparseCore 0:
  10.3 19.4 all-gather.3
  105.4 14.7 all-gather.5
